TPU v7x, 32 devices: a whole 2x2x4 slice. The times are simulated.
32 devices in a mesh: half: 2 (over core), grp: 16 (over z, y, x).
Axes of the slice: x: 2, y: 2, z: 4, core: 2. Of those that a mesh axis runs over, the one named last changes fastest.
Arguments:
- weights: float32 [2, 16, 2, 8192, 128], P('half', 'grp'), may hold values from -4 to 4
- accum: float32 [2, 16, 2, 8192], P('half', 'grp'), may hold values from 0.01 to 1
- grads: float32 [32, 32, 16, 128], P(('half', 'grp')), may hold values from -6 to 6
- row_ids: int32 [32, 32, 16], P(('half', 'grp')), may hold values from 0 to 16383
- counts: int32 [32, 32], P(('half', 'grp')), may hold values from 1 to 16, as said below
Outputs:
- new_weights: float32 [2, 16, 2, 8192, 128], P('half', 'grp')
- new_accum: float32 [2, 16, 2, 8192], P('half', 'grp')
Inputs may be any that keep to these rules, and one draw needn't show every extreme that they name: `counts`: A few owners, the same for all senders, receive 16 live rows from every sender; no two of them share a shard index g (owners g and 16 + g). The owner that shares its shard index with such an owner receives 16 // 2 live rows from every sender; each other count lies from 1 to 8. So the two owners of one shard index receive at most 24 live rows from one sender together, and some pair receives exactly that.
All inputs are finite; a program needn't handle non-finite values.
Results may differ from a plain program's by a relative error of at most 0.00002.
Values sent between devices are 32-bit elements; how exact they have to be, the bound alone decides.
A program may use at most 128 MiB of HBM per device.

v0:
```python
import jax
import jax.numpy as jnp
from jax import lax
from jax.sharding import PartitionSpec as P

LEARN_RATE = 0.5
EPSILON = 1e-06


def partner(value, axis, stride):
    mask = 2**stride
    pairs = [(source, source ^ mask) for source in range(lax.axis_size(axis))]
    return lax.ppermute(value, axis, pairs)


def per_device(weights, accum, grads, row_ids, counts):
    owners = grads.shape[1]
    slots = grads.shape[2]
    width = grads.shape[3]
    rows_half = weights.shape[3]
    top_bit = lax.axis_index("half")
    table = weights[0, 0]
    state = accum[0, 0]
    kept = lax.dynamic_index_in_dim(table, top_bit, 0, keepdims=False)
    given = lax.dynamic_index_in_dim(table, 1 - top_bit, 0, keepdims=False)
    kept_acc = lax.dynamic_index_in_dim(state, top_bit, 0, keepdims=False)
    given_acc = lax.dynamic_index_in_dim(state, 1 - top_bit, 0, keepdims=False)
    gotten, gotten_acc = partner((given, given_acc), "half", 0)
    slot_index = lax.broadcasted_iota(jnp.int32, (owners, slots), 1)
    live = slot_index < counts[0][:, None]
    masked = jnp.where(live[..., None], grads[0], jnp.zeros_like(grads[0]))
    ids_local = row_ids[0]
    received, got_ids = (
        lax.all_to_all(masked, ("half", "grp"), split_axis=0, concat_axis=0, tiled=True),
        lax.all_to_all(ids_local, ("half", "grp"), split_axis=0, concat_axis=0, tiled=True),
    )
    total = (
        jnp.zeros((2 * rows_half, width), jnp.float32)
        .at[got_ids.reshape(-1)]
        .add(received.reshape(-1, width))
    )
    is_low = top_bit == 0
    moved = jnp.where(
        is_low, jnp.concatenate([kept, gotten], 0), jnp.concatenate([gotten, kept], 0)
    )
    moved_acc = jnp.where(
        is_low,
        jnp.concatenate([kept_acc, gotten_acc], 0),
        jnp.concatenate([gotten_acc, kept_acc], 0),
    )
    accumulated = moved_acc + jnp.mean(total * total, axis=-1)
    updated = moved - LEARN_RATE * total / (jnp.sqrt(accumulated)[:, None] + EPSILON)
    return (updated.reshape(1, 1, 2, rows_half, width), accumulated.reshape(1, 1, 2, rows_half))


def solution(mesh):
    placed = (
        P("half", "grp", None, None, None),
        P("half", "grp", None, None),
        P(("half", "grp"), None, None, None),
        P(("half", "grp"), None, None),
        P(("half", "grp"), None),
    )
    return jax.shard_map(
        per_device,
        mesh=mesh,
        in_specs=placed,
        out_specs=(P("half", "grp", None, None, None), P("half", "grp", None, None)),
        check_vma=False,
    )
```

profile of v0, /device:TPU:0, one launch (start us, length us, event | category | flops | bytes accessed | tf_op | source)
XLA Modules:
  0.0 60.9 jit_solution(10767580840746122104)
XLA Ops:
  0.6 0.0 copy-start.2
  0.6 0.0 copy-start.3
  0.7 0.0 copy-start
  0.7 0.0 copy-start.1
  0.7 7.3 %dynamic-slice_bitcast_fusion.1 = (f32[8192,128]{1,0:T(8,128)}, f32[8192,128]{1,0:T(8,128)}) fusion(f32[1,1,2,8192,128]{4,3,2,1,0:T(8,128)} %param.5, s32[]{:T(128)S(6)} %select_n.53, s32[]{:T(128)S(6)} %select_n.54), kind=kLoop, calls=%fused_computation.7 | loop fusion | bytes 16777224 | tf_op jit(solution)/shard_map/jit(dynamic_index_in_dim)/squeeze | solution.py:24
  7.9 0.5 collective-permute-start
  8.4 0.0 copy-done.2
  8.4 0.7 %copy.8 = s32[1,32,16]{2,1,0:T(8,128)} copy(s32[1,32,16]{1,2,0:T(8,128)S(1)} %copy-done.2) | data formatting | bytes 4096 | tf_op args[3]
  9.1 6.9 %all-to-all-start = ((s32[32,1,16]{2,1,0:T(1,128)}), s32[32,1,16]{2,1,0:T(1,128)S(1)}, u32[]{:S(2)}, u32[]{:S(2)}) async-start(s32[32,1,16]{2,1,0:T(1,128)} %bitcast.2), calls=%async_computation | async-start | bytes 32768 | tf_op jit(solution)/shard_map/all_to_all | solution.py:35
  16.1 0.0 copy-done.3
  16.1 0.1 iota_compare_fusion
  16.2 0.0 copy-done
  16.2 0.8 %bitcast_select_fusion = f32[32,16,128]{2,1,0:T(8,128)} fusion(f32[1,32,16,128]{3,2,1,0:T(8,128)S(1)} %copy-done, pred[32,16]{1,0:T(8,128)(4,1)S(1)} %iota_compare_fusion), kind=kLoop, calls=%fused_computation.8 | loop fusion | flops 65536 | bytes 524800 | tf_op jit(solution)/shard_map/jit(_where)/select_n | solution.py:31
  17.0 6.2 %all-to-all-done = s32[32,1,16]{2,1,0:T(1,128)S(1)} async-done(((s32[32,1,16]{2,1,0:T(1,128)}), s32[32,1,16]{2,1,0:T(1,128)S(1)}, u32[]{:S(2)}, u32[]{:S(2)}) %all-to-all-start) | async-done | bytes 2080 | tf_op jit(solution)/shard_map/all_to_all | solution.py:35
  23.1 2.6 %all-to-all-start.1 = ((f32[32,16,128]{2,1,0:T(8,128)}), f32[32,16,128]{2,1,0:T(8,128)S(1)}, u32[]{:S(2)}, u32[]{:S(2)}) async-start(f32[32,16,128]{2,1,0:T(8,128)} %bitcast_select_fusion), calls=%async_computation.1 | async-start | bytes 524288 | tf_op jit(solution)/shard_map/all_to_all | solution.py:34
  25.7 0.0 copy-done.1
  25.8 0.1 constant_dynamic-slice_fusion
  25.8 0.2 collective-permute-start.1
  26.0 0.5 broadcast.60
  26.5 0.7 %reduce.3 = s32[32,16]{1,0:T(8,128)S(1)} reduce(s32[32,1,16]{2,1,0:T(1,128)S(1)} %all-to-all-done, s32[]{:T(128)} %broadcast.60), dimensions={1}, to_apply=%all_to_all.10.reduce_sub_computation.3 | reduce | bytes 4100 | tf_op jit(solution)/shard_map/all_to_all | solution.py:35
  27.2 0.1 reshape.149
  27.3 9.6 %all-to-all-done.1 = f32[32,16,128]{2,1,0:T(8,128)S(1)} async-done(((f32[32,16,128]{2,1,0:T(8,128)}), f32[32,16,128]{2,1,0:T(8,128)S(1)}, u32[]{:S(2)}, u32[]{:S(2)}) %all-to-all-start.1) | async-done | bytes 262176 | tf_op jit(solution)/shard_map/all_to_all | solution.py:34
  36.9 6.1 %scatter_custom_fusion = f32[16384,128]{1,0:T(8,128)} fusion(s32[512]{0:T(512)S(1)} %bitcast.17, f32[512,128]{1,0:T(8,128)S(1)} %bitcast.14, f32[]{:T(128)} %constant.38.clone.1), kind=kCustom, calls=%fused_computation.4 | custom fusion | flops 65536 | bytes 8388612 | tf_op jit(solution)/shard_map/scatter-add | solution.py:40
  43.1 4.6 %multiply_reduce_fusion = f32[16384]{0:T(1024)S(1)} fusion(f32[16384,128]{1,0:T(8,128)} %scatter_custom_fusion), kind=kLoop, calls=%fused_computation.3 | loop fusion | flops 4177920 | bytes 8454144 | tf_op jit(solution)/shard_map/reduce_sum | solution.py:51
  47.7 0.0 collective-permute-done.1
  47.7 0.7 %add.61 = f32[1,1,2,8192]{3,2,1,0:T(2,128)} reshape(f32[16384]{0:T(1024)S(1)} %get-tuple-element.3) | data formatting | bytes 131072 | tf_op jit(solution)/shard_map/add | solution.py:51
  48.4 0.0 collective-permute-done
  48.4 12.5 %fusion = f32[16384,128]{1,0:T(8,128)} fusion(f32[8192,128]{1,0:T(8,128)} %collective-permute-done, f32[8192,128]{1,0:T(8,128)} %get-tuple-element.4, f32[16384,128]{1,0:T(8,128)} %scatter_custom_fusion, f32[16384]{0:T(1024)S(1)} %get-tuple-element.2, pred[]{:T(512)S(6)} %eq.3), kind=kLoop, calls=%fused_computation.2 | loop fusion | flops 12582912 | bytes 25231360 | tf_op jit(solution)/shard_map/sub | solution.py:52
  (2 shorter events, 0.0 us)
Async XLA Ops:
  0.6 7.8 %copy-start.2 = (s32[1,32,16]{1,2,0:T(8,128)S(1)}, s32[1,32,16]{1,2,0:T(8,128)}, u32[]{:S(2)}) copy-start(s32[1,32,16]{1,2,0:T(8,128)} %param.8) | copy-start | bytes 6148
  0.6 15.4 %copy-start.3 = (s32[1,32]{1,0:T(1,128)S(1)}, s32[1,32]{1,0:T(1,128)}, u32[]{:S(2)}) copy-start(s32[1,32]{1,0:T(1,128)} %param.9) | copy-start | bytes 388
  0.7 15.5 %copy-start = (f32[1,32,16,128]{3,2,1,0:T(8,128)S(1)}, f32[1,32,16,128]{3,2,1,0:T(8,128)}, u32[]{:S(2)}) copy-start(f32[1,32,16,128]{3,2,1,0:T(8,128)} %param.7) | copy-start | bytes 786436
  0.7 25.1 %copy-start.1 = (f32[1,1,2,8192]{3,2,1,0:T(2,128)S(1)}, f32[1,1,2,8192]{3,2,1,0:T(2,128)}, u32[]{:S(2)}) copy-start(f32[1,1,2,8192]{3,2,1,0:T(2,128)} %param.6) | copy-start | bytes 196612
  7.9 40.5 %collective-permute-start = (f32[8192,128]{1,0:T(8,128)}, f32[8192,128]{1,0:T(8,128)}, u32[]{:S(2)}, u32[]{:S(2)}) collective-permute-start(f32[8192,128]{1,0:T(8,128)} %get-tuple-element.5), channel_id=1, source_target_pairs={{0,16},{16,0},{1,17},{17,1},{2,18},{18,2},{3,19},{19,3},{4,20},{20... | collective-permute-start | bytes 12582920 | tf_op jit(solution)/shard_map/ppermute | solution.py:13
  9.1 14.0 %all-to-all-start = ((s32[32,1,16]{2,1,0:T(1,128)}), s32[32,1,16]{2,1,0:T(1,128)S(1)}, u32[]{:S(2)}, u32[]{:S(2)}) async-start(s32[32,1,16]{2,1,0:T(1,128)} %bitcast.2), calls=%async_computation | async-start | bytes 32768 | tf_op jit(solution)/shard_map/all_to_all | solution.py:35
  23.1 13.8 %all-to-all-start.1 = ((f32[32,16,128]{2,1,0:T(8,128)}), f32[32,16,128]{2,1,0:T(8,128)S(1)}, u32[]{:S(2)}, u32[]{:S(2)}) async-start(f32[32,16,128]{2,1,0:T(8,128)} %bitcast_select_fusion), calls=%async_computation.1 | async-start | bytes 524288 | tf_op jit(solution)/shard_map/all_to_all | solution.py:34
  25.8 21.9 %collective-permute-start.1 = (f32[8192]{0:T(1024)S(1)}, f32[8192]{0:T(1024)S(1)}, u32[]{:S(2)}, u32[]{:S(2)}) collective-permute-start(f32[8192]{0:T(1024)S(1)} %bitcast.16), channel_id=1, source_target_pairs={{0,16},{16,0},{1,17},{17,1},{2,18},{18,2},{3,19},{19,3},{4,20},{20... | collective-permute-start | bytes 98312 | tf_op jit(solution)/shard_map/ppermute | solution.py:13
where the time goes:
time: 61.2 us; the launch traced here: 60.9 us
  other arithmetic  24.9 us (41%)
  waiting for transfers between devices  15.8 us (26%)
  starting transfers between devices  10.2 us (17%)
  local copies, waits for them, and re-layouts  9.28 us (15%)
  between operations  0.75 us (1%)
    sub x1, other arithmetic, per_device(): moved - LEARN_RATE * total / (jnp.sqrt(accumulated)[:, None] + EPSILON)  12.5 us
    all_to_all x1, waiting for transfers between devices, per_device(): lax.all_to_all(masked, ('half', 'grp'), split_axis=0, concat_axis=0, tile...  9.63 us
    squeeze x1, local copies, waits for them, and re-layouts, per_device(): kept = lax.dynamic_index_in_dim(table, top_bit, 0, keepdims=False)  7.26 us
    all_to_all x1, starting transfers between devices, per_device(): lax.all_to_all(ids_local, ('half', 'grp'), split_axis=0, concat_axis=0, t...  6.95 us
    all_to_all x1, waiting for transfers between devices, per_device(): lax.all_to_all(ids_local, ('half', 'grp'), split_axis=0, concat_axis=0, t...  6.15 us
    scatter-add x1, other arithmetic, per_device(): total = jnp.zeros((2 * rows_half, width), jnp.float32).at[got_ids.reshape...  6.13 us
    reduce_sum x1, other arithmetic, per_device(): accumulated = moved_acc + jnp.mean(total * total, axis=-1)  4.62 us
    all_to_all x1, starting transfers between devices, per_device(): lax.all_to_all(masked, ('half', 'grp'), split_axis=0, concat_axis=0, tile...  2.59 us
  transfers between devices with their start and end apart: 4, of which 2 were waited for; matrix products, arithmetic and copies ran while one was open for 24% of the time, Pallas kernels for 0%

commit v1 on v0

v1 whole, which is shorter than its diff:
```python
import functools

import jax
import jax.numpy as jnp
from jax import lax
from jax.experimental import pallas as pl
from jax.experimental.pallas import tpu as pltpu
from jax.sharding import PartitionSpec as P

LEARN_RATE = 0.5
EPSILON = 1e-06
LANES = 128
MESH = pl.DeviceIdType.MESH
PIECES = 4


def exchange_kernel(
    halves, groups, weights, accum, grads, ids_t, counts,
    gotten, gotten_acc, got, got_ids,
    block_buf, id_pad, id_buf,
    local_sem, row_send, row_recv, acc_send, acc_recv, block_send, block_recv, id_send, id_recv,
):
    half = lax.axis_index("half")
    group = lax.axis_index("grp")
    owners = halves * groups
    me = half * groups + group
    other = 1 - half
    slots = ids_t.shape[0]
    piece = weights.shape[1] // PIECES

    def peer_of(step):
        peer = lax.rem(me + step, owners)
        return peer, (peer // groups, lax.rem(peer, groups))

    barrier = pltpu.get_barrier_semaphore()

    @pl.loop(1, owners)
    def _(step):
        _, where = peer_of(step)
        pl.semaphore_signal(barrier, inc=1, device_id=where, device_id_type=MESH)

    load = pltpu.make_async_copy(grads, block_buf, local_sem.at[0])
    load.start()
    slot = lax.broadcasted_iota(jnp.int32, ids_t.shape, 0)
    id_pad[...] = jnp.full(id_pad.shape, -1, jnp.int32)
    id_pad[0:slots, 0:owners] = jnp.where(slot < counts[...], ids_t[...], -1)
    turned = id_pad[...].T
    for owner in range(owners):
        id_buf[owner, 0:1, :] = turned[owner:owner + 1, :]
    load.wait()
    pl.semaphore_wait(barrier, owners - 1)

    def block_copy(step):
        peer, where = peer_of(step)
        return pltpu.make_async_remote_copy(
            src_ref=block_buf.at[peer], dst_ref=got.at[me],
            send_sem=block_send.at[peer], recv_sem=block_recv.at[me],
            device_id=where, device_id_type=MESH)

    def id_copy(step):
        peer, where = peer_of(step)
        return pltpu.make_async_remote_copy(
            src_ref=id_buf.at[peer], dst_ref=got_ids.at[me],
            send_sem=id_send.at[peer], recv_sem=id_recv.at[me],
            device_id=where, device_id_type=MESH)

    def row_copy(index):
        rows = pl.ds(index * piece, piece)
        return pltpu.make_async_remote_copy(
            src_ref=weights.at[other, rows], dst_ref=gotten.at[rows],
            send_sem=row_send.at[index], recv_sem=row_recv.at[index],
            device_id=(other, group), device_id_type=MESH)

    acc_copy = pltpu.make_async_remote_copy(
        src_ref=accum, dst_ref=gotten_acc, send_sem=acc_send, recv_sem=acc_recv,
        device_id=(other, group), device_id_type=MESH)

    @pl.loop(1, owners)
    def _(step):
        id_copy(step).start()
        block_copy(step).start()

    acc_copy.start()
    for index in range(PIECES):
        row_copy(index).start()
    own_block = pltpu.make_async_copy(block_buf.at[me], got.at[me], local_sem.at[0])
    own_ids = pltpu.make_async_copy(id_buf.at[me], got_ids.at[me], local_sem.at[1])
    own_block.start()
    own_ids.start()
    own_block.wait()
    own_ids.wait()

    @pl.loop(1, owners)
    def _(step):
        id_copy(step).wait_send()
        block_copy(step).wait_send()
        peer, where = peer_of(step)
        pltpu.make_async_remote_copy(
            src_ref=id_buf.at[peer], dst_ref=got_ids.at[peer],
            send_sem=id_send.at[peer], recv_sem=id_recv.at[peer],
            device_id=where, device_id_type=MESH).wait_recv()
        pltpu.make_async_remote_copy(
            src_ref=block_buf.at[peer], dst_ref=got.at[peer],
            send_sem=block_send.at[peer], recv_sem=block_recv.at[peer],
            device_id=where, device_id_type=MESH).wait_recv()

    acc_copy.wait()
    for index in range(PIECES):
        row_copy(index).wait()


def thirds(value):
    first = value.astype(jnp.bfloat16)
    rest = value - first.astype(jnp.float32)
    second = rest.astype(jnp.bfloat16)
    third = (rest - second.astype(jnp.float32)).astype(jnp.bfloat16)
    return jnp.concatenate([first, second, third], axis=1)


def joined(value, width):
    return value[:, 0:width] + value[:, width:2 * width] + value[:, 2 * width:3 * width]


def update_kernel(
    weights, accum, gotten, gotten_acc, got, got_ids, new_weights, new_accum,
    table, state, id_list, picked, delta, in_sem, out_sem, id_sem,
):
    half = lax.axis_index("half")
    senders, slots, width = got.shape
    count = senders * slots
    rows_half = weights.shape[1]
    piece = rows_half // PIECES
    spare = 2 * rows_half
    acc_rows = rows_half // LANES

    ids_in = pltpu.make_async_copy(got_ids, id_list, id_sem)
    ids_in.start()
    loads = []
    for index in range(PIECES):
        rows = pl.ds(index * piece, piece)
        kept_rows = pl.ds(pl.multiple_of(half * rows_half + index * piece, piece), piece)
        gotten_rows = pl.ds(pl.multiple_of((1 - half) * rows_half + index * piece, piece), piece)
        loads.append(pltpu.make_async_copy(
            weights.at[half, rows], table.at[kept_rows], in_sem.at[2 * index]))
        loads.append(pltpu.make_async_copy(
            gotten.at[rows], table.at[gotten_rows], in_sem.at[2 * index + 1]))
    for load in loads:
        load.start()
    table[spare:spare + 8, :] = jnp.zeros((8, width), jnp.float32)

    is_low = half == 0
    own = jnp.where(is_low, accum[0:1, :], accum[1:2, :])
    far = jnp.where(is_low, gotten_acc[0:1, :], gotten_acc[1:2, :])
    for old, line in enumerate((jnp.where(is_low, own, far), jnp.where(is_low, far, own))):
        for row in range(acc_rows):
            at = old * acc_rows + row
            state[at:at + 1, :] = line[:, row * LANES:(row + 1) * LANES]

    lane = lax.broadcasted_iota(jnp.int32, (count, LANES), 1)
    sub = lax.broadcasted_iota(jnp.int32, (count, LANES), 0)
    spread = jnp.broadcast_to(got_ids[...], (senders, slots, LANES)).reshape(count, LANES)
    mine = jnp.where(lane == lax.rem(sub, slots), spread, 0).astype(jnp.float32)
    column = jnp.sum(mine, axis=1, keepdims=True)
    wide = jnp.broadcast_to(column, (count, LANES))
    line = wide.T[0:1, :]
    grad_parts = thirds(got[...].reshape(count, width))
    old_state = state[...]
    state_parts = thirds(old_state)
    lane_f = lane.astype(jnp.float32)
    block = min(count, 512)
    gain = jnp.zeros((2 * acc_rows, 3 * LANES), jnp.float32)
    high_line = jnp.floor(line * (1.0 / LANES))
    for start in range(0, count, block):
        key = column[start:start + block]
        same = key == line
        hot = jnp.where(same, 1.0, 0.0)
        total = joined(jnp.dot(hot.astype(jnp.bfloat16), grad_parts,
                               preferred_element_type=jnp.float32), width)
        at_col = lax.broadcasted_iota(jnp.int32, (block, count), 1)
        at_row = lax.broadcasted_iota(jnp.int32, (block, count), 0) + start
        earlier = jnp.sum(jnp.where(at_col < at_row, hot, 0.0), axis=1, keepdims=True)
        high = jnp.floor(key * (1.0 / LANES))
        low = key - high * LANES
        row_hot = jnp.where(lane_f[:block] == high, 1.0, 0.0).astype(jnp.bfloat16) if acc_rows * 2 == LANES else jnp.where(
            lax.broadcasted_iota(jnp.int32, (block, 2 * acc_rows), 1).astype(jnp.float32) == high, 1.0, 0.0).astype(jnp.bfloat16)
        state_rows = joined(jnp.dot(row_hot, state_parts, preferred_element_type=jnp.float32), LANES)
        at_low = lane_f[:block] == low
        old_acc = jnp.sum(jnp.where(at_low, state_rows, 0.0), axis=1, keepdims=True)
        square = jnp.sum(total * total, axis=1, keepdims=True) * (1.0 / width)
        delta[start:start + block, :] = LEARN_RATE * total / (jnp.sqrt(old_acc + square) + EPSILON)
        once = jnp.where((earlier == 0.0) & (key >= 0.0), square, 0.0)
        add_parts = thirds(jnp.where(at_low, once, 0.0))
        high_of = high_line[:, start:start + block]
        tall = lax.broadcasted_iota(jnp.int32, (2 * acc_rows, block), 0).astype(jnp.float32)
        tall_hot = jnp.where(tall == high_of, 1.0, 0.0).astype(jnp.bfloat16)
        gain = gain + jnp.dot(tall_hot, add_parts, preferred_element_type=jnp.float32)
    state[...] = old_state + joined(gain, LANES)
    for old in range(2):
        for row in range(acc_rows):
            at = old * acc_rows + row
            new_accum[old:old + 1, row * LANES:(row + 1) * LANES] = state[at:at + 1, :]

    ids_in.wait()
    for load in loads:
        load.wait()

    def place(sender, slot):
        at = id_list[sender, 0, slot]
        return jnp.where(at < 0, spare, at)

    @pl.loop(0, senders)
    def _(sender):
        base = pl.multiple_of(sender * slots, slots)
        rows = [table[pl.ds(place(sender, slot), 1), :] for slot in range(slots)]
        for slot in range(slots):
            picked[pl.ds(base + slot, 1), :] = rows[slot]

    picked[...] = picked[...] - delta[...]

    @pl.loop(0, senders)
    def _(sender):
        base = pl.multiple_of(sender * slots, slots)
        rows = [picked[pl.ds(base + slot, 1), :] for slot in range(slots)]
        for slot in range(slots):
            table[pl.ds(place(sender, slot), 1), :] = rows[slot]

    stores = []
    for old in range(2):
        for index in range(PIECES):
            stores.append(pltpu.make_async_copy(
                table.at[pl.ds(old * rows_half + index * piece, piece)],
                new_weights.at[old, pl.ds(index * piece, piece)],
                out_sem.at[old * PIECES + index]))
    for store in stores:
        store.start()
    for store in stores:
        store.wait()


def per_device(halves, groups, weights, accum, grads, row_ids, counts):
    owners, slots, width = grads.shape[1:]
    rows_half = weights.shape[3]
    table = weights[0, 0]
    state = accum[0, 0]
    count = owners * slots
    any_space = pl.BlockSpec(memory_space=pl.ANY)
    vmem = pl.BlockSpec(memory_space=pltpu.VMEM)
    id_width = -(-owners // LANES) * LANES
    dma = pltpu.SemaphoreType.DMA
    gotten, gotten_acc, got, got_ids = pl.pallas_call(
        functools.partial(exchange_kernel, halves, groups),
        out_shape=(
            jax.ShapeDtypeStruct((rows_half, width), jnp.float32),
            jax.ShapeDtypeStruct((2, rows_half), jnp.float32),
            jax.ShapeDtypeStruct((owners, slots, width), jnp.float32),
            jax.ShapeDtypeStruct((owners, 1, LANES), jnp.int32),
        ),
        in_specs=[any_space, vmem, any_space, vmem, vmem],
        out_specs=(any_space, vmem, vmem, vmem),
        scratch_shapes=[
            pltpu.VMEM((owners, slots, width), jnp.float32),
            pltpu.VMEM((LANES, id_width), jnp.int32),
            pltpu.VMEM((owners, 1, LANES), jnp.int32),
            dma((2,)),
            dma((PIECES,)), dma((PIECES,)),
            dma, dma,
            dma((owners,)), dma((owners,)),
            dma((owners,)), dma((owners,)),
        ],
        compiler_params=pltpu.CompilerParams(collective_id=0, has_side_effects=True),
        name="exchange",
    )(table, state, grads[0], row_ids[0].T, counts)
    new_weights, new_accum = pl.pallas_call(
        update_kernel,
        out_shape=(
            jax.ShapeDtypeStruct((2, rows_half, width), jnp.float32),
            jax.ShapeDtypeStruct((2, rows_half), jnp.float32),
        ),
        in_specs=[any_space, vmem, any_space, vmem, vmem, vmem],
        out_specs=(any_space, vmem),
        scratch_shapes=[
            pltpu.VMEM((2 * rows_half + 8, width), jnp.float32),
            pltpu.VMEM((2 * rows_half // LANES, LANES), jnp.float32),
            pltpu.SMEM((owners, 1, LANES), jnp.int32),
            pltpu.VMEM((count, width), jnp.float32),
            pltpu.VMEM((count, width), jnp.float32),
            dma((2 * PIECES,)), dma((2 * PIECES,)), dma,
        ],
        name="update",
    )(table, state, gotten, gotten_acc, got, got_ids)
    return new_weights[None, None], new_accum[None, None]


def solution(mesh):
    placed = (
        P("half", "grp", None, None, None),
        P("half", "grp", None, None),
        P(("half", "grp"), None, None, None),
        P(("half", "grp"), None, None),
        P(("half", "grp"), None),
    )
    return jax.shard_map(
        functools.partial(per_device, mesh.shape["half"], mesh.shape["grp"]),
        mesh=mesh,
        in_specs=placed,
        out_specs=(P("half", "grp", None, None, None), P("half", "grp", None, None)),
        check_vma=False,
    )
```

time: 61.2 us -> 28.6 us (0.47)
  Pallas kernels: 0 us -> 27.8 us
  other arithmetic: 24.9 us -> 0 us
  waiting for transfers between devices: 15.8 us -> 0 us
  starting transfers between devices: 10.2 us -> 0 us
  local copies, waits for them, and re-layouts: 9.28 us -> 0 us
    pallas_call x0 -> x2, Pallas kernels: none -> 27.8 us  [the longest x1 17.6 us: per_device(): pl.pallas_call(functools.partial(exchange_kernel, halves, groups), out_sh...]
    all_to_all x2 -> x0, waiting for transfers between devices: 15.8 us -> none  [the longest x1 9.63 us: per_device(): lax.all_to_all(masked, ('half', 'grp'), split_axis=0, concat_axis=0, tile...]
    sub x1 -> x0, other arithmetic: 12.5 us -> none  [per_device(): moved - LEARN_RATE * total / (jnp.sqrt(accumulated)[:, None] + EPSILON)]
    all_to_all x2 -> x0, starting transfers between devices: 9.53 us -> none  [the longest x1 6.95 us: per_device(): lax.all_to_all(ids_local, ('half', 'grp'), split_axis=0, concat_axis=0, t...]
    squeeze x1 -> x0, local copies, waits for them, and re-layouts: 7.26 us -> none  [per_device(): kept = lax.dynamic_index_in_dim(table, top_bit, 0, keepdims=False)]
    scatter-add x1 -> x0, other arithmetic: 6.13 us -> none  [per_device(): total = jnp.zeros((2 * rows_half, width), jnp.float32).at[got_ids.reshape...]
    reduce_sum x1 -> x0, other arithmetic: 4.62 us -> none  [per_device(): accumulated = moved_acc + jnp.mean(total * total, axis=-1)]
    select_n x2 -> x0, other arithmetic: 0.85 us -> none  [the longest x1 0.84 us: per_device(): masked = jnp.where(live[..., None], grads[0], jnp.zeros_like(grads[0]))]
  transfers between devices with their start and end apart: 4 -> 0, of which waited for: 2 -> 0; matrix products, arithmetic and copies ran while one was open for 24% -> 0% of each run, Pallas kernels for 0% -> 0%
where the time goes in v1:
time: 28.6 us; the launch traced here: 28.4 us
  Pallas kernels  27.8 us (97%)
  between operations  0.64 us (2%)
    pallas_call x1, Pallas kernels, per_device(): pl.pallas_call(functools.partial(exchange_kernel, halves, groups), out_sh...  17.6 us
    pallas_call x1, Pallas kernels, per_device(): pl.pallas_call(update_kernel, out_shape=(jax.ShapeDtypeStruct((2, rows_ha...  10.2 us

profile of v1, /device:TPU:0, one launch (start us, length us, event | category | flops | bytes accessed | tf_op | source)
XLA Modules:
  0.0 28.4 jit_solution(8293707878199186149)
XLA Ops:
  0.6 17.6 %exchange.1 = (f32[8192,128]{1,0:T(8,128)}, f32[2,8192]{1,0:T(2,128)}, f32[32,16,128]{2,1,0:T(8,128)}, s32[32,1,128]{2,1,0:T(1,128)}) custom-call(f32[2,8192,128]{2,1,0:T(8,128)} %bitcast.8, f32[2,8192]{1,0:T(2,128)} %bitcast.10, f32[32,16,128]{2,1,0:T(8,128)} %bitcast.12, s32[16,32]{1,0:T(8,128)} %bitcast.13, s32[1,32]{1,0:T(1,128)} %counts.1), custom_call_target="tpu_custom_call" | custom-call | tf_op jit(solution)/shard_map/exchange/pallas_call | solution.py:250
  18.2 10.2 %update.1 = (f32[2,8192,128]{2,1,0:T(8,128)}, f32[2,8192]{1,0:T(2,128)}) custom-call(f32[2,8192,128]{2,1,0:T(8,128)} %bitcast.9, f32[2,8192]{1,0:T(2,128)} %bitcast.11, f32[8192,128]{1,0:T(8,128)} %get-tuple-element.8.gotten, f32[2,8192]{1,0:T(2,128)} %get-tuple-element.9.gotten_acc, f32[32,16,128]{2,1,0:T(8,128)} %get-tuple-element.10.got, ...), custom_call_target="tpu_custom_call" | custom-call | tf_op jit(solution)/shard_map/update/pallas_call | solution.py:273

commit v2 on v1

--- a/solution.py
+++ b/solution.py
@@ -16,8 +16,8 @@
 
 def exchange_kernel(
     halves, groups, weights, accum, grads, ids_t, counts,
-    gotten, gotten_acc, got, got_ids,
-    block_buf, id_pad, id_buf,
+    table, pair_acc, got, got_ids,
+    block_buf, id_in, count_in, id_pad, id_buf,
     local_sem, row_send, row_recv, acc_send, acc_recv, block_send, block_recv, id_send, id_recv,
 ):
     half = lax.axis_index("half")
@@ -26,7 +26,9 @@
     me = half * groups + group
     other = 1 - half
     slots = ids_t.shape[0]
-    piece = weights.shape[1] // PIECES
+    rows_half = weights.shape[1]
+    piece = rows_half // PIECES
+    home = pl.multiple_of(half * rows_half, rows_half)
 
     def peer_of(step):
         peer = lax.rem(me + step, owners)
@@ -39,11 +41,22 @@
         _, where = peer_of(step)
         pl.semaphore_signal(barrier, inc=1, device_id=where, device_id_type=MESH)
 
+    id_load = pltpu.make_async_copy(ids_t, id_in, local_sem.at[1])
+    count_load = pltpu.make_async_copy(counts, count_in, local_sem.at[2])
     load = pltpu.make_async_copy(grads, block_buf, local_sem.at[0])
+    keep = pltpu.make_async_copy(
+        weights.at[half], table.at[pl.ds(home, rows_half)], local_sem.at[3])
+    keep_acc = pltpu.make_async_copy(accum, pair_acc.at[half], local_sem.at[4])
+    id_load.start()
+    count_load.start()
+    keep_acc.start()
     load.start()
+    keep.start()
+    id_load.wait()
+    count_load.wait()
     slot = lax.broadcasted_iota(jnp.int32, ids_t.shape, 0)
     id_pad[...] = jnp.full(id_pad.shape, -1, jnp.int32)
-    id_pad[0:slots, 0:owners] = jnp.where(slot < counts[...], ids_t[...], -1)
+    id_pad[0:slots, 0:owners] = jnp.where(slot < count_in[...], id_in[...], -1)
     turned = id_pad[...].T
     for owner in range(owners):
         id_buf[owner, 0:1, :] = turned[owner:owner + 1, :]
@@ -67,12 +80,13 @@
     def row_copy(index):
         rows = pl.ds(index * piece, piece)
         return pltpu.make_async_remote_copy(
-            src_ref=weights.at[other, rows], dst_ref=gotten.at[rows],
+            src_ref=weights.at[other, rows],
+            dst_ref=table.at[pl.ds(pl.multiple_of(home + index * piece, piece), piece)],
             send_sem=row_send.at[index], recv_sem=row_recv.at[index],
             device_id=(other, group), device_id_type=MESH)
 
     acc_copy = pltpu.make_async_remote_copy(
-        src_ref=accum, dst_ref=gotten_acc, send_sem=acc_send, recv_sem=acc_recv,
+        src_ref=accum, dst_ref=pair_acc.at[half], send_sem=acc_send, recv_sem=acc_recv,
         device_id=(other, group), device_id_type=MESH)
 
     @pl.loop(1, owners)
@@ -89,6 +103,8 @@
     own_ids.start()
     own_block.wait()
     own_ids.wait()
+    keep.wait()
+    keep_acc.wait()
 
     @pl.loop(1, owners)
     def _(step):
@@ -122,36 +138,24 @@
 
 
 def update_kernel(
-    weights, accum, gotten, gotten_acc, got, got_ids, new_weights, new_accum,
-    table, state, id_list, picked, delta, in_sem, out_sem, id_sem,
+    table_in, pair_acc, got, got_ids, table, new_weights, new_accum,
+    out_acc, state, id_list, picked, delta, in_sem, out_sem, id_sem,
 ):
     half = lax.axis_index("half")
     senders, slots, width = got.shape
     count = senders * slots
-    rows_half = weights.shape[1]
+    rows_half = pair_acc.shape[2]
     piece = rows_half // PIECES
     spare = 2 * rows_half
     acc_rows = rows_half // LANES
 
     ids_in = pltpu.make_async_copy(got_ids, id_list, id_sem)
     ids_in.start()
-    loads = []
-    for index in range(PIECES):
-        rows = pl.ds(index * piece, piece)
-        kept_rows = pl.ds(pl.multiple_of(half * rows_half + index * piece, piece), piece)
-        gotten_rows = pl.ds(pl.multiple_of((1 - half) * rows_half + index * piece, piece), piece)
-        loads.append(pltpu.make_async_copy(
-            weights.at[half, rows], table.at[kept_rows], in_sem.at[2 * index]))
-        loads.append(pltpu.make_async_copy(
-            gotten.at[rows], table.at[gotten_rows], in_sem.at[2 * index + 1]))
-    for load in loads:
-        load.start()
     table[spare:spare + 8, :] = jnp.zeros((8, width), jnp.float32)
 
     is_low = half == 0
-    own = jnp.where(is_low, accum[0:1, :], accum[1:2, :])
-    far = jnp.where(is_low, gotten_acc[0:1, :], gotten_acc[1:2, :])
-    for old, line in enumerate((jnp.where(is_low, own, far), jnp.where(is_low, far, own))):
+    for old in range(2):
+        line = jnp.where(is_low, pair_acc[old, 0:1, :], pair_acc[old, 1:2, :])
         for row in range(acc_rows):
             at = old * acc_rows + row
             state[at:at + 1, :] = line[:, row * LANES:(row + 1) * LANES]
@@ -198,11 +202,11 @@
     for old in range(2):
         for row in range(acc_rows):
             at = old * acc_rows + row
-            new_accum[old:old + 1, row * LANES:(row + 1) * LANES] = state[at:at + 1, :]
-
+            out_acc[old:old + 1, row * LANES:(row + 1) * LANES] = state[at:at + 1, :]
+
+    acc_out = pltpu.make_async_copy(out_acc, new_accum, in_sem)
+    acc_out.start()
     ids_in.wait()
-    for load in loads:
-        load.wait()
 
     def place(sender, slot):
         at = id_list[sender, 0, slot]
@@ -235,6 +239,7 @@
         store.start()
     for store in stores:
         store.wait()
+    acc_out.wait()
 
 
 def per_device(halves, groups, weights, accum, grads, row_ids, counts):
@@ -243,51 +248,59 @@
     table = weights[0, 0]
     state = accum[0, 0]
     count = owners * slots
-    any_space = pl.BlockSpec(memory_space=pl.ANY)
+    hbm = pl.BlockSpec(memory_space=pltpu.HBM)
     vmem = pl.BlockSpec(memory_space=pltpu.VMEM)
     id_width = -(-owners // LANES) * LANES
     dma = pltpu.SemaphoreType.DMA
-    gotten, gotten_acc, got, got_ids = pl.pallas_call(
+    landed = (
+        jax.ShapeDtypeStruct((2 * rows_half + 8, width), jnp.float32),
+        jax.ShapeDtypeStruct((2, 2, rows_half), jnp.float32),
+        jax.ShapeDtypeStruct((owners, slots, width), jnp.float32),
+        jax.ShapeDtypeStruct((owners, 1, LANES), jnp.int32),
+    )
+    moved, pair_acc, got, got_ids = pl.pallas_call(
         functools.partial(exchange_kernel, halves, groups),
-        out_shape=(
-            jax.ShapeDtypeStruct((rows_half, width), jnp.float32),
-            jax.ShapeDtypeStruct((2, rows_half), jnp.float32),
-            jax.ShapeDtypeStruct((owners, slots, width), jnp.float32),
-            jax.ShapeDtypeStruct((owners, 1, LANES), jnp.int32),
-        ),
-        in_specs=[any_space, vmem, any_space, vmem, vmem],
-        out_specs=(any_space, vmem, vmem, vmem),
+        out_shape=landed,
+        in_specs=[hbm] * 5,
+        out_specs=(vmem,) * 4,
         scratch_shapes=[
             pltpu.VMEM((owners, slots, width), jnp.float32),
+            pltpu.VMEM((slots, owners), jnp.int32),
+            pltpu.VMEM((1, owners), jnp.int32),
             pltpu.VMEM((LANES, id_width), jnp.int32),
             pltpu.VMEM((owners, 1, LANES), jnp.int32),
-            dma((2,)),
+            dma((5,)),
             dma((PIECES,)), dma((PIECES,)),
             dma, dma,
             dma((owners,)), dma((owners,)),
             dma((owners,)), dma((owners,)),
         ],
-        compiler_params=pltpu.CompilerParams(collective_id=0, has_side_effects=True),
+        compiler_params=pltpu.CompilerParams(
+            collective_id=0, has_side_effects=True, vmem_limit_bytes=16 << 20),
         name="exchange",
-    )(table, state, grads[0], row_ids[0].T, counts)
-    new_weights, new_accum = pl.pallas_call(
+    )(*(pltpu.with_memory_space_constraint(value, pltpu.HBM)
+        for value in (table, state, grads[0], row_ids[0].T, counts)))
+    _, new_weights, new_accum = pl.pallas_call(
         update_kernel,
         out_shape=(
+            jax.ShapeDtypeStruct((2 * rows_half + 8, width), jnp.float32),
             jax.ShapeDtypeStruct((2, rows_half, width), jnp.float32),
             jax.ShapeDtypeStruct((2, rows_half), jnp.float32),
         ),
-        in_specs=[any_space, vmem, any_space, vmem, vmem, vmem],
-        out_specs=(any_space, vmem),
+        in_specs=[vmem] * 4,
+        out_specs=(vmem, hbm, hbm),
         scratch_shapes=[
-            pltpu.VMEM((2 * rows_half + 8, width), jnp.float32),
+            pltpu.VMEM((2, rows_half), jnp.float32),
             pltpu.VMEM((2 * rows_half // LANES, LANES), jnp.float32),
             pltpu.SMEM((owners, 1, LANES), jnp.int32),
             pltpu.VMEM((count, width), jnp.float32),
             pltpu.VMEM((count, width), jnp.float32),
-            dma((2 * PIECES,)), dma((2 * PIECES,)), dma,
+            dma, dma((2 * PIECES,)), dma,
         ],
+        input_output_aliases={0: 0},
+        compiler_params=pltpu.CompilerParams(vmem_limit_bytes=32 << 20),
         name="update",
-    )(table, state, gotten, gotten_acc, got, got_ids)
+    )(moved, pair_acc, got, got_ids)
     return new_weights[None, None], new_accum[None, None]
 
 

time: 28.6 us -> 23.3 us (0.81)
  Pallas kernels: 27.8 us -> 22.5 us
    pallas_call x1, Pallas kernels: 10.2 us -> 6.15 us  [per_device(): pl.pallas_call(update_kernel, out_shape=(jax.ShapeDtypeStruct((2 * rows_h...]
    pallas_call x1, Pallas kernels: 17.6 us -> 16.3 us  [per_device(): pl.pallas_call(functools.partial(exchange_kernel, halves, groups), out_sh...]
where the time goes in v2:
time: 23.3 us; the launch traced here: 23.1 us
  Pallas kernels  22.5 us (97%)
  between operations  0.64 us (3%)
    pallas_call x1, Pallas kernels, per_device(): pl.pallas_call(functools.partial(exchange_kernel, halves, groups), out_sh...  16.3 us
    pallas_call x1, Pallas kernels, per_device(): pl.pallas_call(update_kernel, out_shape=(jax.ShapeDtypeStruct((2 * rows_h...  6.15 us

profile of v2, /device:TPU:0, one launch (start us, length us, event | category | flops | bytes accessed | tf_op | source)
XLA Modules:
  0.0 23.1 jit_solution(3516684785238067607)
XLA Ops:
  0.6 16.3 %exchange.1 = (f32[16392,128]{1,0:T(8,128)S(1)}, f32[2,2,8192]{2,1,0:T(2,128)S(1)}, f32[32,16,128]{2,1,0:T(8,128)S(1)}, s32[32,1,128]{2,1,0:T(1,128)S(1)}) custom-call(f32[2,8192,128]{2,1,0:T(8,128)} %bitcast.8, f32[2,8192]{1,0:T(2,128)} %bitcast.10, f32[32,16,128]{2,1,0:T(8,128)} %bitcast.9, s32[16,32]{1,0:T(8,128)} %bitcast.11, s32[1,32]{1,0:T(1,128)} %counts.1), custom_call_target="tpu_custom_call" | custom-call | tf_op jit(solution)/shard_map/exchange/pallas_call | solution.py:261
  17.0 6.1 %update.1 = (f32[16392,128]{1,0:T(8,128)S(1)}, f32[2,8192,128]{2,1,0:T(8,128)}, f32[2,8192]{1,0:T(2,128)}) custom-call(f32[16392,128]{1,0:T(8,128)S(1)} %get-tuple-element.8.table_in, f32[2,2,8192]{2,1,0:T(2,128)S(1)} %get-tuple-element.9.pair_acc, f32[32,16,128]{2,1,0:T(8,128)S(1)} %get-tuple-element.10.got, ...), custom_call_target="tpu_custom_call", output_to_operand_aliasing={{0}: (0, {})} | custom-call | tf_op jit(solution)/shard_map/update/pallas_call | solution.py:283
